TPU v7x, 128 devices: a whole 4x4x4 slice. The times are simulated.
128 devices in a mesh: tasks: 1, col: 2 (over core), row: 64 (over z, y, x).
Axes of the slice: x: 4, y: 4, z: 4, core: 2. Of those that a mesh axis runs over, the one named last changes fastest.
Arguments:
- x_pts: bfloat16 [98304, 128], P(('tasks', 'row', 'col'))
- v_rhs: bfloat16 [98304, 32], P(('tasks', 'row', 'col'))
- length_scale: float32 [1], replicated
- out_scale: float32 [1], replicated
Outputs:
- output: float32 [98304, 32], P(('tasks', 'row', 'col'))
All inputs are finite; a program needn't handle non-finite values.
Results may differ from a plain program's by a relative error of at most 0.001.
Values are sent between devices in bfloat16 or wider.
A program may use at most 1 GiB of HBM per device.

v0:
```python
import jax
import jax.numpy as jnp
from jax import lax
from jax.sharding import PartitionSpec as P


def tile_product(x_tgt, n_tgt, x_src, n_src, v_src, two_ell_sq, scale_val):
    gram_mat = jnp.einsum("id,jd->ij", x_tgt, x_src, preferred_element_type=jnp.float32)
    sq_dist = jnp.maximum(n_tgt[:, None] + n_src[None, :] - 2.0 * gram_mat, 0.0)
    kern_bf = (scale_val * jnp.exp(-sq_dist / two_ell_sq)).astype(jnp.bfloat16)
    return jnp.dot(kern_bf, v_src, preferred_element_type=jnp.float32)


def kernel_rows(x_tgt, x_src, v_src, two_ell_sq, scale_val, tile_rows):
    feat_dim = x_tgt.shape[1]
    rhs_dim = v_src.shape[1]
    n_tgt_blocks = x_tgt.shape[0] // tile_rows
    n_src_blocks = x_src.shape[0] // tile_rows
    tgt_norms = jnp.sum(jnp.square(x_tgt.astype(jnp.float32)), axis=1)
    src_norms = jnp.sum(jnp.square(x_src.astype(jnp.float32)), axis=1)
    tgt_blocks = x_tgt.reshape(n_tgt_blocks, tile_rows, feat_dim)
    tgt_norm_blocks = tgt_norms.reshape(n_tgt_blocks, tile_rows)

    def target_rows(tgt_pair):
        x_blk, n_blk = tgt_pair

        def src_step(src_idx, acc_rows):
            row_start = src_idx * tile_rows
            x_part = lax.dynamic_slice_in_dim(x_src, row_start, tile_rows, axis=0)
            n_part = lax.dynamic_slice_in_dim(src_norms, row_start, tile_rows, axis=0)
            v_part = lax.dynamic_slice_in_dim(v_src, row_start, tile_rows, axis=0)
            return acc_rows + tile_product(x_blk, n_blk, x_part, n_part, v_part, two_ell_sq, scale_val)

        return lax.fori_loop(0, n_src_blocks, src_step, jnp.zeros((tile_rows, rhs_dim), jnp.float32))

    y_blocks = lax.map(target_rows, (tgt_blocks, tgt_norm_blocks))
    return y_blocks.reshape(n_tgt_blocks * tile_rows, rhs_dim)


def solution(mesh):
    def local_rows(x_loc, v_loc, length_scale, out_scale):
        tile_rows = x_loc.shape[0]
        two_ell_sq = 2.0 * length_scale[0] * length_scale[0]
        x_tgt = lax.all_gather(x_loc, "col", axis=0, tiled=True)
        x_src = lax.all_gather(x_loc, "row", axis=0, tiled=True)
        v_src = lax.all_gather(v_loc, "row", axis=0, tiled=True)
        y_part = kernel_rows(x_tgt, x_src, v_src, two_ell_sq, out_scale[0], tile_rows)
        return lax.psum_scatter(y_part, "col", scatter_dimension=0, tiled=True)

    row_spec = P(("tasks", "row", "col"), None)
    rep_spec = P(None)
    return jax.shard_map(local_rows, mesh=mesh, in_specs=(row_spec, row_spec, rep_spec, rep_spec), out_specs=row_spec, check_vma=False)
```

profile of v0, /device:TPU:1, one launch (start us, length us, event | category | flops | bytes accessed | tf_op | source)
XLA Modules:
  0.0 577.4 jit_solution(4271025078501562516)
XLA Ops:
  9.7 3.1 all_gather.9
  13.0 90.7 %all-gather.3.cloned.1.call-done = bf16[49152,128]{1,0:T(8,128)(2,1)} async-done(((bf16[768,128]{1,0:T(8,128)(2,1)}), bf16[49152,128]{1,0:T(8,128)(2,1)}) %all-gather.3.cloned.1.call-update) | async-done | bytes 12582928 | tf_op jit(solution)/shard_map/all_gather | solution.py:45
  103.8 9.6 %multiply_reduce_fusion = f32[49152]{0:T(1024)S(1)} fusion(bf16[49152,128]{1,0:T(8,128)(2,1)} %all-gather.3.cloned.1.call-done), kind=kLoop, calls=%fused_computation.22 | loop fusion | flops 18825216 | bytes 12779520 | tf_op jit(solution)/shard_map/reduce_sum | solution.py:20
  113.4 83.4 %all-gather.5.cloned.1.call-done = bf16[49152,32]{1,0:T(8,128)(2,1)} async-done(((bf16[768,32]{1,0:T(8,128)(2,1)}), bf16[49152,32]{1,0:T(8,128)(2,1)}) %all-gather.5.cloned.1.call-update) | async-done | bytes 3145744 | tf_op jit(solution)/shard_map/all_gather | solution.py:46
  196.8 362.6 %while.25 = (s32[]{:T(128)}, f32[2,768,32]{1,0,2:T(2,128)S(1)}, bf16[2,768,128]{2,1,0:T(8,128)(2,1)S(1)}, f32[2,768]{1,0:T(2,128)S(1)}, f32[]{:T(128)}, /*index=...) while((s32[]{:T(128)}, f32[2,768,32]{1,0,2:T(2,128)S(1)}, ...), condition=%wide.region_5.6_spmd, body=%wide.region_2.5_spmd.sunk | while | flops 193511424 | bytes 1594305 | solution.py:36
  196.9 179.6 %while.26 = (s32[]{:T(128)}, f32[768,32]{0,1:T(8,128)S(1)}, f32[]{:T(128)}, f32[768]{0:T(1024)S(1)}, f32[49152]{0:T(1024)S(1)}, /*index=5*/bf16[49152,128]{1,0:T...) while((s32[]{:T(128)}, f32[768,32]{0,1:T(8,128)S(1)}, ...), condition=%wide.region_4.4_spmd.clone, body=%wide.region_3.3_spmd.clone.sunk | while | flops 193511424 | bytes 801464 | solution.py:34
  199.8 2.7 fusion.29
  211.0 2.7 fusion.29
  213.8 2.7 fusion.29
  216.6 2.7 fusion.29
  227.9 2.7 fusion.29
  230.7 2.7 fusion.29
  233.5 2.7 fusion.29
  236.3 2.7 fusion.29
  244.7 2.7 fusion.29
  250.3 2.7 fusion.29
  261.5 2.7 fusion.29
  264.3 2.7 fusion.29
  267.1 2.7 fusion.29
  281.2 2.7 fusion.29
  284.0 2.7 fusion.29
  286.8 2.7 fusion.29
  378.2 179.6 %while.26 = (s32[]{:T(128)}, f32[768,32]{0,1:T(8,128)S(1)}, f32[]{:T(128)}, f32[768]{0:T(1024)S(1)}, f32[49152]{0:T(1024)S(1)}, /*index=5*/bf16[49152,128]{1,0:T...) while((s32[]{:T(128)}, f32[768,32]{0,1:T(8,128)S(1)}, ...), condition=%wide.region_4.4_spmd.clone, body=%wide.region_3.3_spmd.clone.sunk | while | flops 193511424 | bytes 801464 | solution.py:34
  560.2 10.7 %reduce-scatter.2.cloned.1.call-done = f32[768,32]{0,1:T(8,128)} async-done(((f32[1536,32]{0,1:T(8,128)}), f32[768,32]{0,1:T(8,128)}) %reduce-scatter.2.cloned.1.call-update) | async-done | bytes 98320 | tf_op jit(solution)/shard_map/reduce_scatter | solution.py:48
  (261 shorter events, 319.0 us)
Async XLA Ops:
  6.5 97.2 %all-gather.3.cloned.1.call-start = ((), (), s32[]{:S(2)}) async-start(), calls=%async_computation.1 | async-start | bytes 12779520 | tf_op jit(solution)/shard_map/all_gather | solution.py:45
  7.3 189.6 %all-gather.5.cloned.1.call-start = ((), (), s32[]{:S(2)}) async-start(), calls=%async_computation.2 | async-start | bytes 12779520 | tf_op jit(solution)/shard_map/all_gather | solution.py:46
  9.0 561.9 %reduce-scatter.2.cloned.1.call-start = ((), (), s32[]{:S(2)}) async-start(), calls=%async_computation.3 | async-start | bytes 294912 | tf_op jit(solution)/shard_map/reduce_scatter | solution.py:48
Sparse Core Ops, SparseCore 0:
  10.1 93.6 all-gather.2
  106.5 90.2 all-gather.4
  560.3 10.5 reduce-scatter.1
where the time goes:
time: 581 us; the launch traced here: 577 us
  matrix products  345 us (59%)
  waiting for transfers between devices  186 us (32%)
  local copies, waits for them, and re-layouts  15.8 us (3%)
  between operations  13.8 us (2%)
  other arithmetic  9.89 us (2%)
    dot_general x128, matrix products, tile_product(): return jnp.dot(kern_bf, v_src, preferred_element_type=jnp.float32)  345 us
    all_gather x1, waiting for transfers between devices, local_rows(): x_src = lax.all_gather(x_loc, 'row', axis=0, tiled=True)  90.7 us
    all_gather x1, waiting for transfers between devices, local_rows(): v_src = lax.all_gather(v_loc, 'row', axis=0, tiled=True)  83.4 us
  transfers between devices with their start and end apart: 3, of which 3 were waited for; matrix products, arithmetic and copies ran while one was open for 2% of the time, Pallas kernels for 0%

commit v1 on v0

v1 whole, which is shorter than its diff:
```python
import functools

import jax
import jax.numpy as jnp
from jax import lax
from jax.experimental import pallas as pl
from jax.experimental.pallas import tpu as pltpu
from jax.sharding import PartitionSpec as P

BF = jnp.bfloat16
F32 = jnp.float32
ROWS = 768
FEAT = 128
RHS = 32
NSRC = 32
NTGT = 4
GROUPS = 6
VROWS = GROUPS * RHS
SROWS = ROWS + VROWS
XROWS = 144
TILES = 3
STEPS = 24
PAIRS = 6
TRIPS = NSRC * TILES // STEPS
LOG2E = 1.4426950408889634
BIG = 3.0e38


def pieces(norm):
    half = jnp.maximum(norm * -0.5, -BIG)
    hi = half.astype(BF).astype(F32)
    rest = half - hi
    mid = rest.astype(BF).astype(F32)
    return hi, mid, rest - mid


def select(pos, at, vals):
    out = jnp.zeros_like(vals[0] + pos.astype(F32))
    for k, val in enumerate(vals):
        out = jnp.where(pos == at + k, val, out)
    return out


def position():
    col = lax.axis_index("col")
    row = lax.axis_index("row")
    return col, row // 16, (row // 4) % 4, row % 4


def device(col, z, y, x):
    return (0, col, (z % 4) * 16 + (y % 4) * 4 + x % 4)


def enter(peers):
    barrier = pltpu.get_barrier_semaphore()
    for peer in peers:
        pl.semaphore_signal(barrier, inc=1, device_id=peer, device_id_type=pl.DeviceIdType.MESH)
    pl.semaphore_wait(barrier, len(peers))


def gather_kernel(x_ref, v_ref, sx_ref, aug_ref, xt_ref, ssem, rsem, tsend, trecv):
    c, z, y, x = position()
    partner = device(1 - c, z, y, x)

    sx_ref[0, 0:ROWS, :] = x_ref[...]
    for g in range(GROUPS):
        sx_ref[0, ROWS + g * RHS : ROWS + (g + 1) * RHS, :] = v_ref[:, g * 128 : (g + 1) * 128]
    xt = jnp.transpose(x_ref[...].astype(F32))
    nrm = jnp.sum(xt * xt, axis=0, keepdims=True)
    hi, mid, low = pieces(nrm)
    pos = lax.broadcasted_iota(jnp.int32, (16, 128), 0)
    for g in range(GROUPS):
        s = slice(g * 128, (g + 1) * 128)
        xt_ref[0, g, 0:FEAT, :] = xt[:, s].astype(BF)
        one = jnp.ones((1, 128), F32)
        xt_ref[0, g, FEAT:XROWS, :] = select(pos, 0, (hi[:, s], mid[:, s], low[:, s], one, one, one)).astype(BF)

    enter([partner, device(c, z + 1, y, x), device(c, z + 3, y, x), device(c, z, y + 1, x),
           device(c, z, y + 3, x), device(c, z, y, x + 1), device(c, z, y, x + 3)])

    copies = []

    def send(src, dst, dev):
        cp = pltpu.make_async_remote_copy(sx_ref.at[src], sx_ref.at[dst], ssem.at[len(copies)], rsem.at[dst],
                                          device_id=dev, device_id_type=pl.DeviceIdType.MESH)
        cp.start()
        copies.append(cp)

    def got(slot):
        pltpu.make_async_remote_copy(sx_ref.at[slot], sx_ref.at[slot], ssem.at[0], rsem.at[slot],
                                     device_id=partner, device_id_type=pl.DeviceIdType.MESH).wait_recv()

    tcopies = []

    def tsnd(src, dst, dev):
        cp = pltpu.make_async_remote_copy(xt_ref.at[src, :, pl.ds(0, XROWS), :], xt_ref.at[dst, :, pl.ds(0, XROWS), :],
                                          tsend.at[len(tcopies)], trecv.at[dst],
                                          device_id=dev, device_id_type=pl.DeviceIdType.MESH)
        cp.start()
        tcopies.append(cp)

    def tgot(slot):
        pltpu.make_async_remote_copy(xt_ref.at[slot, :, pl.ds(0, XROWS), :], xt_ref.at[slot, :, pl.ds(0, XROWS), :],
                                     tsend.at[0], trecv.at[slot],
                                     device_id=partner, device_id_type=pl.DeviceIdType.MESH).wait_recv()

    def pos_slot(dz, dy):
        return (dz * 4 + dy) * 2

    lane = lax.broadcasted_iota(jnp.int32, (128, 128), 1)

    def build(slot):
        def chunk(i, carry):
            rows = pl.ds(pl.multiple_of(i * 128, 128), 128)
            xs = sx_ref[slot, rows, :].astype(F32)
            nj = jnp.sum(xs * xs, axis=1, keepdims=True)
            hi, mid, low = pieces(nj)
            one = jnp.ones((128, 1), F32)
            aug_ref[slot, rows, :] = select(lane, 0, (one, one, one, hi, mid, low)).astype(BF)
            return carry

        lax.fori_loop(0, ROWS // 128, chunk, 0)

    sgn = 1 - 2 * c
    send(pos_slot(0, 0), pos_slot(3, 0), device(c, z + 1, y, x))
    send(pos_slot(0, 0), pos_slot(1, 0), device(c, z + 3, y, x))
    send(pos_slot(0, 0), pos_slot(0, 3), device(c, z, y + 1, x))
    send(pos_slot(0, 0), pos_slot(0, 1), device(c, z, y + 3, x))
    tsnd(0, 3, device(c, z, y, x + 1))
    tsnd(0, 1, device(c, z, y, x + 3))
    send(pos_slot(0, 0), 1, partner)
    for t in range(NTGT):
        for g in range(GROUPS):
            xt_ref[t, g, XROWS:256, :] = jnp.zeros((256 - XROWS, 128), BF)
    build(0)
    got(1)
    build(1)

    near = 2 + sgn
    far = 2 - sgn
    got(pos_slot(near, 0))
    send(pos_slot(near, 0), pos_slot(2, 0), device(c, z + sgn, y, x))
    got(pos_slot(0, near))
    send(pos_slot(0, near), pos_slot(0, 2), device(c, z, y + sgn, x))
    tgot(2 + sgn)
    tsnd(2 + sgn, 2, device(c, z, y, x + sgn))
    got(pos_slot(far, 0))
    got(pos_slot(0, far))

    def cross(k, m):
        return (k * (4 - 3 * c) + m * (1 + 3 * c)) * 2

    def ahead(d):
        return device(c, z + d * c, y + d * (1 - c), x)

    def pass_on(k):
        send(cross(k, 0), cross(k, 3), ahead(1))
        send(cross(k, 0), cross(k, 1), ahead(3))

    def share(slot):
        send(slot, slot + 1, partner)

    pass_on(1)
    pass_on(3)
    for s in (pos_slot(1, 0), pos_slot(3, 0), pos_slot(0, 1), pos_slot(0, 3)):
        share(s)
        build(s)
    got(pos_slot(2, 0))
    got(pos_slot(0, 2))
    pass_on(2)
    for s in (pos_slot(2, 0), pos_slot(0, 2)):
        share(s)
        build(s)
    for s in (pos_slot(1, 0), pos_slot(3, 0), pos_slot(0, 1), pos_slot(0, 3), pos_slot(2, 0), pos_slot(0, 2)):
        got(s + 1)
        build(s + 1)
    for k, d in ((1, 1), (3, 3), (2, 1)):
        a = 2 + d if d == 1 else 1
        b = 4 - a
        got(cross(k, a))
        send(cross(k, a), cross(k, 2), ahead(d))
        share(cross(k, a))
        build(cross(k, a))
        got(cross(k, b))
        share(cross(k, b))
        build(cross(k, b))
    for k in (1, 3, 2):
        got(cross(k, 2))
        share(cross(k, 2))
        build(cross(k, 2))
    for k in (1, 3, 2):
        for m in (1, 3, 2):
            got(pos_slot(k, m) + 1)
            build(pos_slot(k, m) + 1)
    tgot(2 - sgn)
    tgot(2)
    for cp in copies:
        cp.wait_send()
    for cp in tcopies:
        cp.wait_send()


def product_kernel(sc_ref, sx_ref, aug_ref, xt_ref, y_ref, tile_ref):
    alpha = sc_ref[0]
    scale = sc_ref[1]
    piece = 64
    n_pc = 256 // piece

    def run(*accs):
        per = 3 * n_pc + 2
        gram = [[[accs[q * per + r * n_pc + p] for p in range(n_pc)] for r in range(3)] for q in range(2)]
        body_acc = [accs[q * per + 3 * n_pc] for q in range(2)]
        tail_acc = [accs[q * per + 3 * n_pc + 1] for q in range(2)]

        def acc_gram(q, u, blk, tile, p):
            rows = pl.ds(tile * 256 + p * piece, piece)
            lhs = jnp.concatenate([sx_ref[blk, rows, :], aug_ref[blk, rows, :]], axis=1)
            pltpu.matmul_acc_lhs(gram[q][u % 3][p], lhs, load_staged_rhs=0 if p == 0 else None)

        def push_x(q, pair):
            tgt = (pair // 3) * 2 + q
            ch = (pair % 3) * 2
            pltpu.matmul_push_rhs(jnp.concatenate([xt_ref[tgt, ch], xt_ref[tgt, ch + 1]], axis=1),
                                  staging_register=0, mxu_index=q)

        def push_tile(q, u):
            pltpu.matmul_push_rhs(tile_ref[q, (u - 1) % 2], staging_register=1, mxu_index=q)

        def values(q, u, p):
            half = pltpu.matmul_pop(gram[q][(u - 2) % 3][p])
            kern = (jnp.exp2(jnp.minimum(half * alpha, 0.0)) * scale).astype(BF)
            tile_ref[q, u % 2, p * piece : (p + 1) * piece, :] = kern

        def acc_y(q, u, blk, tile, acc):
            lo = ROWS + tile * 2 * RHS
            vt = jnp.concatenate([sx_ref[blk, lo : lo + RHS, :], sx_ref[blk, lo + RHS : lo + 2 * RHS, :]], axis=1)
            pltpu.matmul_acc_lhs(acc[q], vt, load_staged_rhs=1)

        def add_y(acc, pair):
            for q in range(2):
                y_ref[(pair // 3) * 2 + q, pair % 3] += pltpu.matmul_pop(acc[q])

        def trip(k, carry):
            pair = k // TRIPS
            blk0 = (k % TRIPS) * (STEPS // TILES)
            last = k + TRIPS * PAIRS - 1
            old_blk0 = (last % TRIPS) * (STEPS // TILES)
            old_pair = jnp.where(k == 0, PAIRS, (k - 1) // TRIPS)
            for u in range(STEPS):
                blk, tile = blk0 + u // TILES, u % TILES
                nxt = pair if u < STEPS - 1 else jnp.minimum((k + 1) // TRIPS, PAIRS - 1)
                for q in range(2):
                    push_tile(q, u)
                for p in range(n_pc):
                    for q in range(2):
                        acc_gram(q, u, blk, tile, p)
                        if p == 0:
                            push_x(q, nxt)
                    for q in range(2):
                        values(q, u, p)
                for q in range(2):
                    if u < 3:
                        w = STEPS - 3 + u
                        acc_y(q, u, old_blk0 + w // TILES, w % TILES, tail_acc)
                    else:
                        w = u - 3
                        acc_y(q, u, blk0 + w // TILES, w % TILES, body_acc)
                if u == 1:
                    add_y(body_acc, old_pair)
                if u == 6:
                    add_y(tail_acc, old_pair)
            return carry

        for q in range(2):
            for r in range(3):
                for p in range(n_pc):
                    pltpu.matmul_pop(gram[q][r][p])
            pltpu.matmul_pop(body_acc[q])
            pltpu.matmul_pop(tail_acc[q])
            push_x(q, 0)
        y_ref[...] = jnp.zeros_like(y_ref)
        lax.fori_loop(0, TRIPS * PAIRS, trip, 0)
        for u in range(STEPS, STEPS + 3):
            w = u - 3
            for q in range(2):
                push_tile(q, u)
                if u < STEPS + 2:
                    for p in range(n_pc):
                        values(q, u, p)
                acc_y(q, u, NSRC - STEPS // TILES + w // TILES, w % TILES, tail_acc)
        add_y(body_acc, PAIRS - 1)
        for q in range(2):
            acc_gram(q, 0, 0, 0, 0)
            pltpu.matmul_pop(gram[q][0][0])
        add_y(tail_acc, PAIRS - 1)

    specs = []
    for q in range(2):
        specs += [pltpu.ACC(q)((piece, 256), F32)] * (3 * n_pc) + [pltpu.ACC(q)((RHS, 256), F32)] * 2
    pl.run_scoped(run, *specs)


def reduce_kernel(yp_ref, y_ref, got_ref, ssem, rsem):
    c, z, y, x = position()
    enter([device(c, z, y, x + d) for d in (1, 2, 3)])
    copies = []
    for d in (2, 1, 3):
        cp = pltpu.make_async_remote_copy(yp_ref.at[d], got_ref.at[d - 1], ssem.at[d - 1], rsem.at[d - 1],
                                          device_id=device(c, z, y, x + d), device_id_type=pl.DeviceIdType.MESH)
        cp.start()
        copies.append(cp)
    for cp in copies:
        cp.wait()
    for ch in range(3):
        tot = yp_ref[0, ch] + got_ref[0, ch] + got_ref[1, ch] + got_ref[2, ch]
        y_ref[:, ch * 256 : (ch + 1) * 256] = tot


VM = pl.BlockSpec(memory_space=pltpu.VMEM)
SM = pl.BlockSpec(memory_space=pltpu.SMEM)


def solution(mesh):
    def local_rows(x_loc, v_loc, length_scale, out_scale):
        two_ell_sq = 2.0 * length_scale[0] * length_scale[0]
        consts = jnp.stack([(2.0 * LOG2E) / two_ell_sq, out_scale[0]])
        sx, aug, xt = pl.pallas_call(
            gather_kernel,
            out_shape=(jax.ShapeDtypeStruct((NSRC, SROWS, 128), BF), jax.ShapeDtypeStruct((NSRC, ROWS, 128), BF),
                       jax.ShapeDtypeStruct((NTGT, GROUPS, 256, 128), BF)),
            in_specs=[VM, VM],
            out_specs=(VM, VM, VM),
            scratch_shapes=[pltpu.SemaphoreType.DMA((40,)), pltpu.SemaphoreType.DMA((NSRC,)),
                            pltpu.SemaphoreType.DMA((4,)), pltpu.SemaphoreType.DMA((NTGT,))],
            compiler_params=pltpu.CompilerParams(collective_id=0, has_side_effects=True, vmem_limit_bytes=24 * 2**20),
            name="gather",
        )(x_loc, v_loc.T)
        yp = pl.pallas_call(
            product_kernel,
            out_shape=jax.ShapeDtypeStruct((6, 3, RHS, 256), F32),
            in_specs=[SM, VM, VM, VM],
            out_specs=VM,
            scratch_shapes=[pltpu.VMEM((2, 2, 256, 256), BF)],
            compiler_params=pltpu.CompilerParams(vmem_limit_bytes=24 * 2**20),
            name="product",
        )(consts, sx, aug, xt)
        y_t = pl.pallas_call(
            reduce_kernel,
            out_shape=jax.ShapeDtypeStruct((RHS, ROWS), F32),
            in_specs=[VM],
            out_specs=VM,
            scratch_shapes=[pltpu.VMEM((3, 3, RHS, 256), F32), pltpu.SemaphoreType.DMA((3,)), pltpu.SemaphoreType.DMA((3,))],
            compiler_params=pltpu.CompilerParams(collective_id=1, has_side_effects=True, vmem_limit_bytes=8 * 2**20),
            name="reduce",
        )(yp)
        return y_t.T

    row_spec = P(("tasks", "row", "col"), None)
    rep_spec = P(None)
    return jax.shard_map(local_rows, mesh=mesh, in_specs=(row_spec, row_spec, rep_spec, rep_spec), out_specs=row_spec, check_vma=False)
```

time: 581 us -> 104 us (0.18)
  the two profiles are of different devices: /device:TPU:1 before, /device:TPU:0 now
where the time goes in v1:
time: 104 us
  Pallas kernels  100 us (96%)
  local copies, waits for them, and re-layouts  2.37 us (2%)
  between operations  1.36 us (1%)
    pallas_call x1, Pallas kernels, local_rows(): pl.pallas_call(product_kernel, out_shape=jax.ShapeDtypeStruct((6, 3, RHS,...  51 us
    pallas_call x1, Pallas kernels, local_rows(): pl.pallas_call(gather_kernel, out_shape=(jax.ShapeDtypeStruct((NSRC, SROW...  42.2 us
    pallas_call x1, Pallas kernels, local_rows(): pl.pallas_call(reduce_kernel, out_shape=jax.ShapeDtypeStruct((RHS, ROWS),...  7.07 us
    unnamed x5, local copies, waits for them, and re-layouts  2.37 us

profile of v1, /device:TPU:0, one launch (start us, length us, event | category | flops | bytes accessed | tf_op | source)
XLA Modules:
  0.0 104.1 jit_solution(11149061438206378004)
XLA Ops:
  1.3 0.1 pad_maximum_fusion.sc_ref
  1.4 0.0 copy-start
  1.4 0.9 copy-done
  2.3 0.0 copy-start.1
  2.3 0.8 copy-done.1
  3.1 42.2 %gather.1 = (bf16[32,960,128]{2,1,0:T(8,128)(2,1)S(1)}, bf16[32,768,128]{2,1,0:T(8,128)(2,1)S(1)}, bf16[4,6,256,128]{3,2,1,0:T(8,128)(2,1)S(1)}) custom-call(bf16[768,128]{1,0:T(8,128)(2,1)S(1)} %copy-done, bf16[32,768]{1,0:T(8,128)(2,1)S(1)} %bitcast.7), custom_call_target="tpu_custom_call" | custom-call | tf_op jit(solution)/shard_map/gather/pallas_call | solution.py:327
  45.3 51.0 %product.1.yp_ref = f32[6,3,32,256]{3,2,1,0:T(8,128)S(1)} custom-call(f32[2]{0:T(128)S(1)} %pad_maximum_fusion.sc_ref, bf16[32,960,128]{2,1,0:T(8,128)(2,1)S(1)} %get-tuple-element.8.sx_ref, bf16[32,768,128]{2,1,0:T(8,128)(2,1)S(1)} %get-tuple-element.9.aug_ref, bf16[4,6,256,128]{3,2,1,0:T(8,128)(2,1)S(1)} %get-tuple-element.10.xt_ref), custom_call_target="tpu_custom_call" | custom-call | tf_op jit(solution)/shard_map/product/pallas_call | solution.py:338
  96.4 7.1 %reduce.1 = f32[32,768]{1,0:T(8,128)S(1)} custom-call(f32[6,3,32,256]{3,2,1,0:T(8,128)S(1)} %product.1.yp_ref), custom_call_target="tpu_custom_call" | custom-call | tf_op jit(solution)/shard_map/reduce/pallas_call | solution.py:347
  103.5 0.6 copy.8
Async XLA Ops:
  1.4 0.9 copy-start
  2.3 0.8 copy-start.1
